TPU v7x, 32 devices: a whole 2x2x4 slice. The times are simulated.
32 devices in a mesh: enc: 8 (over z, x), section: 2 (over core), llmdp: 2 (over y).
Axes of the slice: x: 2, y: 2, z: 4, core: 2. Of those that a mesh axis runs over, the one named last changes fastest.
Arguments:
- patches: bfloat16 [2048, 3200], P('enc', ('section', 'llmdp')), may hold values from -6 to 6
- gain: float32 [3200], replicated, may hold values from 0.25 to 1.75
- shift: float32 [3200], replicated, may hold values from -3 to 3
- proj_weight: bfloat16 [3200, 8192], P('enc', ('section', 'llmdp')), may hold values from -0.109375 to 0.109375
- llm_rank: int32 [2048, 1], P('enc'), may hold values from 0 to 7; in each aligned block of 256 rows (0 to 255, 256 to 511, ...) at most 96 rows name the same one
- embed_grad: bfloat16 [6144, 8192], P('enc', ('section', 'llmdp')), may hold values from -0.59765625 to 0.59765625
Outputs:
- embeds_recv: bfloat16 [6144, 8192], P('enc', ('section', 'llmdp'))
- hidden_state_gradient: bfloat16 [2048, 3200], P('enc', ('section', 'llmdp'))
- grad_weight: float32 [3200, 8192], P('enc', ('section', 'llmdp'))
- gain_gradient: float32 [3200], P(('section', 'llmdp'))
- grad_shift: float32 [3200], P(('section', 'llmdp'))
Inputs may be any that keep to these rules, and one draw needn't show every extreme that they name: `llm_rank`: among the 256 rows of one device, at most 96 name the same owner, a bound that some block reaches.
All inputs are finite; a program needn't handle non-finite values.
Results may differ from a plain program's by a relative error of at most 0.018.
Values may be sent and summed in bfloat16 or wider, within the bound.
A program may use at most 128 MiB of HBM per device.

v0:
```python
import jax
import jax.numpy as jnp
from jax import lax
from jax.sharding import PartitionSpec as P

EPSILON = 1e-05


def body(patches, gain, shift, proj_weight, llm_rank, embed_grad):
    row_count = patches.shape[0]
    owned_width = patches.shape[1]
    width = gain.shape[0]
    out_cols = proj_weight.shape[1]
    column_start = lax.axis_index(("section", "llmdp")) * owned_width
    gain_own = lax.dynamic_slice_in_dim(gain, column_start, owned_width, 0)
    complete_rows = lax.all_gather(patches, ("section", "llmdp"), axis=1, tiled=True).astype(
        jnp.float32
    )
    row_average = jnp.mean(complete_rows, 1, keepdims=True)
    variance = jnp.mean(complete_rows * complete_rows, 1, keepdims=True) - row_average * row_average
    inverse_deviation = lax.rsqrt(variance + EPSILON)
    standardized_full = (complete_rows - row_average) * inverse_deviation
    normed_hidden = (standardized_full * gain + shift).astype(jnp.bfloat16)
    standardized_owned = lax.dynamic_slice_in_dim(standardized_full, column_start, owned_width, 1)
    weight_full = lax.all_gather(proj_weight, "enc", axis=0, tiled=True)
    embed_acc = jnp.dot(normed_hidden, weight_full, preferred_element_type=jnp.float32)
    embed = embed_acc.astype(jnp.bfloat16)
    senders = lax.axis_size("enc")
    most_slots = embed_grad.shape[0] // senders
    target = llm_rank[:, 0]
    owners = jnp.arange(senders, dtype=jnp.int32)
    hits = (target[:, None] == owners[None, :]).astype(jnp.int32)
    rank = jnp.sum((jnp.cumsum(hits, 0) - hits) * hits, 1)
    slot = target * most_slots + rank
    outgoing = jnp.zeros((senders * most_slots, out_cols), jnp.bfloat16).at[slot].set(embed)
    arrived = lax.all_to_all(
        outgoing.reshape(senders, most_slots, out_cols),
        "enc",
        split_axis=0,
        concat_axis=0,
        tiled=True,
    )
    embeds_recv = arrived.reshape(senders * most_slots, out_cols)
    returned = lax.all_to_all(
        embed_grad.reshape(senders, most_slots, out_cols),
        "enc",
        split_axis=0,
        concat_axis=0,
        tiled=True,
    )
    d_embed = returned.reshape(senders * most_slots, out_cols)[slot]
    partial_grad = lax.dot_general(
        d_embed, weight_full, (((1,), (1,)), ((), ())), preferred_element_type=jnp.float32
    )
    grad_weight = lax.psum_scatter(
        lax.dot_general(
            normed_hidden, d_embed, (((0,), (0,)), ((), ())), preferred_element_type=jnp.float32
        ).astype(jnp.bfloat16),
        "enc",
        scatter_dimension=0,
        tiled=True,
    ).astype(jnp.float32)
    group_count = width // owned_width
    pieces = partial_grad.astype(jnp.bfloat16).reshape(row_count, group_count, owned_width)
    columns = lax.all_to_all(pieces, ("section", "llmdp"), split_axis=1, concat_axis=1, tiled=True)
    owned_normalized_gradient = jnp.sum(columns.astype(jnp.float32), 1)
    owned_centered_gradient = owned_normalized_gradient * gain_own
    mean_sum, cross_sum = lax.psum(
        (
            jnp.sum(owned_centered_gradient, 1),
            jnp.sum(owned_centered_gradient * standardized_owned, 1),
        ),
        ("section", "llmdp"),
    )
    gradient_row_average = (mean_sum / width)[:, None]
    gradient_cross_product = (cross_sum / width)[:, None]
    hidden_state_gradient = (
        inverse_deviation
        * (
            owned_centered_gradient
            - gradient_row_average
            - standardized_owned * gradient_cross_product
        )
    ).astype(jnp.bfloat16)
    gain_gradient, grad_shift = lax.psum(
        (
            jnp.sum(owned_normalized_gradient * standardized_owned, 0),
            jnp.sum(owned_normalized_gradient, 0),
        ),
        "enc",
    )
    return (embeds_recv, hidden_state_gradient, grad_weight, gain_gradient, grad_shift)


def solution(mesh):
    in_specs = (
        P("enc", ("section", "llmdp")),
        P(),
        P(),
        P("enc", ("section", "llmdp")),
        P("enc", None),
        P("enc", ("section", "llmdp")),
    )
    out_specs = (
        P("enc", ("section", "llmdp")),
        P("enc", ("section", "llmdp")),
        P("enc", ("section", "llmdp")),
        P(("section", "llmdp")),
        P(("section", "llmdp")),
    )
    return jax.shard_map(body, mesh=mesh, in_specs=in_specs, out_specs=out_specs, check_vma=False)
```

profile of v0, /device:TPU:0, one launch (start us, length us, event | category | flops | bytes accessed | tf_op | source)
XLA Modules:
  0.0 557.3 jit_solution(7519992521454355701)
XLA Ops:
  7.2 0.7 all-gather.3.cloned.1.call-update
  7.9 0.7 all-gather.5.cloned.1.call-update
  8.7 7.3 %all-to-all-start.1 = ((bf16[8,96,2048]{2,1,0:T(8,128)(2,1)}), bf16[8,96,2048]{2,1,0:T(8,128)(2,1)S(1)}, u32[]{:S(2)}, u32[]{:S(2)}) async-start(bf16[8,96,2048]{2,1,0:T(8,128)(2,1)} %bitcast.25), calls=%async_computation.1 | async-start | bytes 6291456 | tf_op jit(solution)/shard_map/all_to_all | solution.py:44
  17.0 15.3 %all-gather.3.cloned.1.call-done = bf16[256,3200]{0,1:T(8,128)(2,1)} async-done(((bf16[256,800]{0,1:T(8,128)(2,1)}), bf16[256,3200]{0,1:T(8,128)(2,1)}) %all-gather.3.cloned.1.call-update) | async-done | bytes 1638416 | tf_op jit(solution)/shard_map/all_gather | solution.py:16
  32.3 1.9 convert_reduce_fusion
  34.2 96.0 %all-to-all-done.1 = bf16[8,96,2048]{2,1,0:T(8,128)(2,1)S(1)} async-done(((bf16[8,96,2048]{2,1,0:T(8,128)(2,1)}), bf16[8,96,2048]{2,1,0:T(8,128)(2,1)S(1)}, u32[]{:S(2)}, u32[]{:S(2)}) %all-to-all-start.1) | async-done | bytes 3145760 | tf_op jit(solution)/shard_map/all_to_all | solution.py:44
  130.2 2.3 gather_fusion
  132.5 8.7 %convolution_convert_fusion = bf16[3200,2048]{1,0:T(8,128)(2,1)} fusion(bf16[256,2048]{1,0:T(8,128)(2,1)} %gather_fusion, f32[3200]{0:T(1024)S(1)} %copy-done.4, f32[3200]{0:T(1024)S(1)} %copy-done.3, f32[256]{0:T(256)S(1)} %get-tuple-element.17, f32[256]{0:T(256)S(1)} %get-tuple-element.16, bf16[256,3200]{0,1:T(8,128)(2,1)} %all-gather.3.cloned.1.call-done), kind=kOutput, calls=%fused_computation.2 | convolution fusion | flops 3366912000 | bytes 15821824 | tf_op jit(solution)/shard_map/dot_general | solution.py:56
  141.2 114.2 %all-gather.5.cloned.1.call-done = bf16[3200,2048]{1,0:T(8,128)(2,1)} async-done(((bf16[400,2048]{1,0:T(8,128)(2,1)}), bf16[3200,2048]{1,0:T(8,128)(2,1)}) %all-gather.5.cloned.1.call-update) | async-done | bytes 13107216 | tf_op jit(solution)/shard_map/all_gather | solution.py:25
  255.4 8.4 %convolution_convert_fusion.1 = bf16[256,3200]{1,0:T(8,128)(2,1)S(1)} fusion(bf16[256,2048]{1,0:T(8,128)(2,1)S(1)} %copy-done.2, bf16[3200,2048]{1,0:T(8,128)(2,1)} %all-gather.5.cloned.1.call-done), kind=kOutput, calls=%fused_computation.3 | convolution fusion | flops 3356262400 | bytes 15794176 | tf_op jit(solution)/shard_map/dot_general | solution.py:52
  263.9 2.2 copy.11
  266.2 3.7 all-to-all-start.2
  269.9 9.6 %convolution_convert_fusion.2 = bf16[256,2048]{1,0:T(8,128)(2,1)} fusion(bf16[3200,2048]{1,0:T(8,128)(2,1)} %all-gather.5.cloned.1.call-done, f32[3200]{0:T(1024)S(1)} %copy-done.4, f32[3200]{0:T(1024)S(1)} %copy-done.3, f32[256]{0:T(256)S(1)} %get-tuple-element.17, f32[256]{0:T(256)S(1)} %get-tuple-element.16, bf16[256,3200]{0,1:T(8,128)(2,1)S(1)} %copy-done), kind=kOutput, calls=%fused_computation.12 | convolution fusion | flops 3360882688 | bytes 15821824 | tf_op jit(solution)/shard_map/dot_general | solution.py:26
  279.5 5.0 scatter_custom_fusion
  284.5 6.0 %all-to-all-done.2 = bf16[256,4,800]{0,2,1:T(8,128)(2,1)S(1)} async-done(((bf16[256,4,800]{0,2,1:T(8,128)(2,1)}), bf16[256,4,800]{0,2,1:T(8,128)(2,1)S(1)}, u32[]{:S(2)}, u32[]{:S(2)}) %all-to-all-start.2) | async-done | bytes 1638432 | tf_op jit(solution)/shard_map/all_to_all | solution.py:65
  290.5 4.5 all-to-all-start
  295.7 1.4 copy-done.1
  297.4 6.3 %all-reduce.1 = (f32[256]{0:T(256)S(1)}, f32[256]{0:T(256)S(1)}) all-reduce(f32[256]{0:T(256)S(1)} %get-tuple-element.6, f32[256]{0:T(256)S(1)} %get-tuple-element.11), channel_id=1, replica_groups=mesh['enc'=8,'section'=2,'llmdp'=2] {'section','llmdp'}, use_global_device_ids=true, to_apply=%region_10.11 | all-reduce | flops 512 | bytes 4096 | tf_op jit(solution)/shard_map/psum | solution.py:68
  303.8 109.9 %all-reduce = (f32[800]{0:T(1024)}, f32[800]{0:T(1024)}) all-reduce(f32[800]{0:T(1024)S(1)} %get-tuple-element.5, f32[800]{0:T(1024)S(1)} %get-tuple-element.7), channel_id=1, replica_groups=mesh['enc'=8,'section'=2,'llmdp'=2] {'enc'}, use_global_device_ids=true, to_apply=%region_13.14 | all-reduce | flops 1600 | bytes 12800 | tf_op jit(solution)/shard_map/psum | solution.py:85
  413.7 2.1 multiply_convert_fusion
  415.8 22.0 %all-to-all-done = bf16[8,96,2048]{2,1,0:T(8,128)(2,1)} async-done(((bf16[8,96,2048]{2,1,0:T(8,128)(2,1)}), bf16[8,96,2048]{2,1,0:T(8,128)(2,1)}, u32[]{:S(2)}, u32[]{:S(2)}) %all-to-all-start) | async-done | bytes 3145760 | tf_op jit(solution)/shard_map/all_to_all | solution.py:36
  437.8 105.5 %reduce-scatter.2.cloned.1.call-done = bf16[400,2048]{1,0:T(8,128)(2,1)} async-done(((bf16[3200,2048]{1,0:T(8,128)(2,1)}), bf16[400,2048]{1,0:T(8,128)(2,1)}) %reduce-scatter.2.cloned.1.call-update) | async-done | bytes 1638416 | tf_op jit(solution)/shard_map/reduce_scatter | solution.py:55
  543.2 3.5 convert_element_type.40
  546.8 4.0 copy.13
  (29 shorter events, 2.2 us)
Async XLA Ops:
  7.2 25.1 %all-gather.3.cloned.1.call-start = ((), (), s32[]{:S(2)}) async-start(), calls=%async_computation.4 | async-start | bytes 2048000 | tf_op jit(solution)/shard_map/all_gather | solution.py:16
  7.9 247.5 %all-gather.5.cloned.1.call-start = ((), (), s32[]{:S(2)}) async-start(), calls=%async_computation.5 | async-start | bytes 14745600 | tf_op jit(solution)/shard_map/all_gather | solution.py:25
  8.6 7.4 %copy-start.5 = (s32[256,1]{0,1:T(1,128)S(1)}, s32[256,1]{0,1:T(1,128)}, u32[]{:S(2)}) copy-start(s32[256,1]{0,1:T(1,128)} %param.10) | copy-start | bytes 3076
  8.7 121.5 %all-to-all-start.1 = ((bf16[8,96,2048]{2,1,0:T(8,128)(2,1)}), bf16[8,96,2048]{2,1,0:T(8,128)(2,1)S(1)}, u32[]{:S(2)}, u32[]{:S(2)}) async-start(bf16[8,96,2048]{2,1,0:T(8,128)(2,1)} %bitcast.25), calls=%async_computation.1 | async-start | bytes 6291456 | tf_op jit(solution)/shard_map/all_to_all | solution.py:44
  16.0 527.3 %reduce-scatter.2.cloned.1.call-start = ((), (), s32[]{:S(2)}) async-start(), calls=%async_computation.6 | async-start | bytes 14745600 | tf_op jit(solution)/shard_map/reduce_scatter | solution.py:55
  130.2 2.3 copy-start.3
  130.2 2.3 copy-start.4
  141.2 114.2 %copy-start.2 = (bf16[256,2048]{1,0:T(8,128)(2,1)S(1)}, bf16[256,2048]{1,0:T(8,128)(2,1)}, u32[]{:S(2)}) copy-start(bf16[256,2048]{1,0:T(8,128)(2,1)} %gather_fusion) | copy-start | bytes 3145732
  263.9 6.0 %copy-start = (bf16[256,3200]{0,1:T(8,128)(2,1)S(1)}, bf16[256,3200]{0,1:T(8,128)(2,1)}, u32[]{:S(2)}) copy-start(bf16[256,3200]{0,1:T(8,128)(2,1)} %all-gather.3.cloned.1.call-done) | copy-start | bytes 4915204
  266.2 24.3 %all-to-all-start.2 = ((bf16[256,4,800]{0,2,1:T(8,128)(2,1)}), bf16[256,4,800]{0,2,1:T(8,128)(2,1)S(1)}, u32[]{:S(2)}, u32[]{:S(2)}) async-start(bf16[256,4,800]{0,2,1:T(8,128)(2,1)} %bitcast.24), calls=%async_computation.2 | async-start | bytes 3276800 | tf_op jit(solution)/shard_map/all_to_all | solution.py:65
  290.5 147.3 %all-to-all-start = ((bf16[8,96,2048]{2,1,0:T(8,128)(2,1)}), bf16[8,96,2048]{2,1,0:T(8,128)(2,1)}, u32[]{:S(2)}, u32[]{:S(2)}) async-start(bf16[8,96,2048]{2,1,0:T(8,128)(2,1)} %bitcast.23), calls=%async_computation | async-start | bytes 6291456 | tf_op jit(solution)/shard_map/all_to_all | solution.py:36
  295.4 1.7 copy-start.1
Sparse Core Ops, SparseCore 0:
  9.5 22.7 all-gather.2
  34.5 220.9 all-gather.4
  259.1 284.0 reduce-scatter.1
where the time goes:
time: 558 us; the launch traced here: 557 us
  waiting for transfers between devices  360 us (65%)
  blocking collectives  116 us (21%)
  matrix products  26.7 us (5%)
  starting transfers between devices  15.6 us (3%)
  local copies, waits for them, and re-layouts  15.2 us (3%)
  between operations  13.9 us (2%)
  other arithmetic  9.31 us (2%)
    all_gather x1, waiting for transfers between devices, body(): weight_full = lax.all_gather(proj_weight, 'enc', axis=0, tiled=True)  114 us
    psum x1, blocking collectives, body(): lax.psum((jnp.sum(owned_normalized_gradient * standardized_owned, 0), jnp...  110 us
    reduce_scatter x1, waiting for transfers between devices, body(): lax.psum_scatter(lax.dot_general(normed_hidden, d_embed, (((0,), (0,)), (...  105 us
    all_to_all x1, waiting for transfers between devices, body(): lax.all_to_all(embed_grad.reshape(senders, most_slots, out_cols), 'enc',...  96 us
    all_to_all x1, waiting for transfers between devices, body(): lax.all_to_all(outgoing.reshape(senders, most_slots, out_cols), 'enc', sp...  22 us
    all_gather x1, waiting for transfers between devices, body(): lax.all_gather(patches, ('section', 'llmdp'), axis=1, tiled=True)  15.3 us
  transfers between devices with their start and end apart: 6, of which 6 were waited for; matrix products, arithmetic and copies ran while one was open for 8% of the time, Pallas kernels for 0%

commit v1 on v0

v1 whole, which is shorter than its diff:
```python
import jax
import jax.numpy as jnp
from jax import lax
from jax.sharding import PartitionSpec as P

EPSILON = 1e-05


MAX_BLOCK = 2


def block_size(senders, out_cols):
    size = MAX_BLOCK
    while size > 1 and (senders % size or senders == size or out_cols % (size * 128)):
        size //= 2
    return size


def body(patches, gain, shift, proj_weight, llm_rank, embed_grad):
    features = ("section", "llmdp")
    own_rows, owned_width = patches.shape
    width = gain.shape[0]
    weight_rows, out_cols = proj_weight.shape
    senders = lax.axis_size("enc")
    block = block_size(senders, out_cols)
    near = [[b * block + i for i in range(block)] for b in range(senders // block)]
    far = [[b * block + i for b in range(senders // block)] for i in range(block)]

    def near_exchange(x, split, concat):
        return lax.all_to_all(x, "enc", split, concat, axis_index_groups=near, tiled=True)

    column_start = lax.axis_index(features) * owned_width
    gain_own = lax.dynamic_slice_in_dim(gain, column_start, owned_width, 0)

    weight_part = near_exchange(proj_weight, 1, 0)
    weight = lax.all_gather(weight_part, "enc", axis=0, axis_index_groups=far, tiled=True)

    block_rows = lax.all_gather(patches, "enc", axis=0, axis_index_groups=near, tiled=True)
    complete_rows = lax.all_gather(block_rows, features, axis=1, tiled=True).astype(jnp.float32)
    row_average = jnp.mean(complete_rows, 1, keepdims=True)
    variance = jnp.mean(complete_rows * complete_rows, 1, keepdims=True) - row_average * row_average
    inverse_deviation = lax.rsqrt(variance + EPSILON)
    standardized = (complete_rows - row_average) * inverse_deviation
    normed = (standardized * gain + shift).astype(jnp.bfloat16)

    row_start = (lax.axis_index("enc") % block) * own_rows
    average_own = lax.dynamic_slice_in_dim(row_average, row_start, own_rows, 0)
    deviation_own = lax.dynamic_slice_in_dim(inverse_deviation, row_start, own_rows, 0)
    standardized_owned = (patches.astype(jnp.float32) - average_own) * deviation_own

    most_slots = embed_grad.shape[0] // senders
    target = llm_rank[:, 0]
    owners = jnp.arange(senders, dtype=jnp.int32)
    hits = (target[:, None] == owners[None, :]).astype(jnp.int32)
    rank = jnp.sum((jnp.cumsum(hits, 0) - hits) * hits, 1)
    slot = target * most_slots + rank

    def enc_exchange(x):
        return lax.all_to_all(
            x.reshape(senders, most_slots, out_cols), "enc", split_axis=0, concat_axis=0, tiled=True
        ).reshape(senders * most_slots, out_cols)

    d_embed = near_exchange(enc_exchange(embed_grad)[slot], 1, 0)
    grad_part = lax.psum_scatter(
        lax.dot_general(
            normed, d_embed, (((0,), (0,)), ((), ())), preferred_element_type=jnp.float32
        ).astype(jnp.bfloat16),
        "enc",
        scatter_dimension=0,
        axis_index_groups=far,
        tiled=True,
    )
    grad_weight = near_exchange(grad_part, 0, 1).astype(jnp.float32)

    embed_part = jnp.dot(normed, weight, preferred_element_type=jnp.float32).astype(jnp.bfloat16)
    embed = near_exchange(embed_part, 0, 1)
    outgoing = jnp.zeros((senders * most_slots, out_cols), jnp.bfloat16).at[slot].set(embed)
    embeds_recv = enc_exchange(outgoing)

    partial_grad = lax.dot_general(
        d_embed, weight, (((1,), (1,)), ((), ())), preferred_element_type=jnp.float32
    )
    group_count = width // owned_width
    pieces = partial_grad.astype(jnp.bfloat16).reshape(block * own_rows, group_count, owned_width)
    columns = lax.all_to_all(pieces, features, split_axis=1, concat_axis=1, tiled=True)
    column_sum = jnp.sum(columns.astype(jnp.float32), 1).astype(jnp.bfloat16)
    shares = near_exchange(column_sum.reshape(block, own_rows, owned_width), 0, 0)
    owned_normalized_gradient = jnp.sum(shares.astype(jnp.float32), 0)
    owned_centered_gradient = owned_normalized_gradient * gain_own
    mean_sum, cross_sum = lax.psum(
        (
            jnp.sum(owned_centered_gradient, 1),
            jnp.sum(owned_centered_gradient * standardized_owned, 1),
        ),
        features,
    )
    gradient_row_average = (mean_sum / width)[:, None]
    gradient_cross_product = (cross_sum / width)[:, None]
    hidden_state_gradient = (
        deviation_own
        * (
            owned_centered_gradient
            - gradient_row_average
            - standardized_owned * gradient_cross_product
        )
    ).astype(jnp.bfloat16)
    gain_gradient, grad_shift = lax.psum(
        (
            jnp.sum(owned_normalized_gradient * standardized_owned, 0),
            jnp.sum(owned_normalized_gradient, 0),
        ),
        "enc",
    )
    return (embeds_recv, hidden_state_gradient, grad_weight, gain_gradient, grad_shift)


def solution(mesh):
    in_specs = (
        P("enc", ("section", "llmdp")),
        P(),
        P(),
        P("enc", ("section", "llmdp")),
        P("enc", None),
        P("enc", ("section", "llmdp")),
    )
    out_specs = (
        P("enc", ("section", "llmdp")),
        P("enc", ("section", "llmdp")),
        P("enc", ("section", "llmdp")),
        P(("section", "llmdp")),
        P(("section", "llmdp")),
    )
    return jax.shard_map(body, mesh=mesh, in_specs=in_specs, out_specs=out_specs, check_vma=False)
```

time: 558 us -> 468 us (0.84)
  waiting for transfers between devices: 360 us -> 279 us
  blocking collectives: 116 us -> 67.3 us
  starting transfers between devices: 15.6 us -> 40.5 us
  local copies, waits for them, and re-layouts: 15.2 us -> 29.5 us
    all_to_all x3 -> x7, waiting for transfers between devices: 124 us -> 276 us  [the longest x2 227 us: enc_exchange(): lax.all_to_all(x.reshape(senders, most_slots, out_cols), 'enc', split_axi...]
    all_gather x2, waiting for transfers between devices: 130 us -> 2.23 us  [the longest x1 2.23 us: body(): lax.all_gather(weight_part, 'enc', axis=0, axis_index_groups=far, tiled=T...]
    reduce_scatter x1, waiting for transfers between devices: 105 us -> 0.01 us  [body(): lax.psum_scatter(lax.dot_general(normed, d_embed, (((0,), (0,)), ((), ())...]
    psum x1, blocking collectives: 110 us -> 20.9 us  [body(): lax.psum((jnp.sum(owned_normalized_gradient * standardized_owned, 0), jnp...]
    all_to_all x3 -> x7, starting transfers between devices: 15.5 us -> 40.4 us  [the longest x4 22.3 us: near_exchange(): lax.all_to_all(x, 'enc', split, concat, axis_index_groups=near, tiled=True)]
    all_to_all x0 -> x1, blocking collectives: none -> 23 us  [near_exchange(): lax.all_to_all(x, 'enc', split, concat, axis_index_groups=near, tiled=True)]
    all_gather x0 -> x1, blocking collectives: none -> 15.1 us  [body(): lax.all_gather(patches, 'enc', axis=0, axis_index_groups=near, tiled=True)]
    all_to_all x0 -> x4, local copies, waits for them, and re-layouts: none -> 7.67 us  [near_exchange(): lax.all_to_all(x, 'enc', split, concat, axis_index_groups=near, tiled=True)]
  transfers between devices with their start and end apart: 6 -> 10, of which waited for: 6 -> 7; matrix products, arithmetic and copies ran while one was open for 8% -> 13% of each run, Pallas kernels for 0% -> 0%
where the time goes in v1:
time: 468 us; the launch traced here: 467 us
  waiting for transfers between devices  279 us (60%)
  blocking collectives  67.3 us (14%)
  starting transfers between devices  40.5 us (9%)
  local copies, waits for them, and re-layouts  29.5 us (6%)
  matrix products  23.1 us (5%)
  between operations  13.9 us (3%)
  other arithmetic  13.7 us (3%)
    all_to_all x2, waiting for transfers between devices, enc_exchange(): lax.all_to_all(x.reshape(senders, most_slots, out_cols), 'enc', split_axi...  227 us
    all_to_all x1, waiting for transfers between devices, body(): lax.all_to_all(pieces, features, split_axis=1, concat_axis=1, tiled=True)  27.1 us
    all_to_all x1, blocking collectives, near_exchange(): lax.all_to_all(x, 'enc', split, concat, axis_index_groups=near, tiled=True)  23 us
    all_to_all x4, starting transfers between devices, near_exchange(): lax.all_to_all(x, 'enc', split, concat, axis_index_groups=near, tiled=True)  22.3 us
    all_to_all x4, waiting for transfers between devices, near_exchange(): lax.all_to_all(x, 'enc', split, concat, axis_index_groups=near, tiled=True)  22.2 us
    psum x1, blocking collectives, body(): lax.psum((jnp.sum(owned_normalized_gradient * standardized_owned, 0), jnp...  20.9 us
    all_gather x1, blocking collectives, body(): lax.all_gather(patches, 'enc', axis=0, axis_index_groups=near, tiled=True)  15.1 us
    all_to_all x2, starting transfers between devices, enc_exchange(): lax.all_to_all(x.reshape(senders, most_slots, out_cols), 'enc', split_axi...  14.2 us
  transfers between devices with their start and end apart: 10, of which 7 were waited for; matrix products, arithmetic and copies ran while one was open for 13% of the time, Pallas kernels for 0%

profile of v1, /device:TPU:0, one launch (start us, length us, event | category | flops | bytes accessed | tf_op | source)
XLA Modules:
  0.0 466.7 jit_solution(16512288865410212296)
XLA Ops:
  7.2 15.1 %all_gather.9 = bf16[512,800]{0,1:T(8,128)(2,1)} all-gather(bf16[256,800]{0,1:T(8,128)(2,1)} %param.6), channel_id=1, replica_groups={{0,4},{8,12},{16,20},{24,28},{1,5},{9,13},{17,21},{25,29},{2,6},{10,14}..., dimensions={0}, use_global_device_ids=true | all-gather | bytes 1228800 | tf_op jit(solution)/shard_map/all_gather | solution.py:38
  24.0 23.0 %all_to_all.90 = bf16[400,2,1024]{2,0,1:T(8,128)(2,1)} all-to-all(bf16[400,2,1024]{2,0,1:T(8,128)(2,1)S(1)} %bitcast.54), channel_id=1, replica_groups={{0,4},{8,12},{16,20},{24,28},{1,5},{9,13},{17,21},{25,29},{2,6},{10,14}..., dimensions={1} | all-to-all | bytes 3276800 | tf_op jit(solution)/shard_map/all_to_all | solution.py:30
  47.0 4.9 %all-to-all-start.3 = ((bf16[8,96,2048]{2,1,0:T(8,128)(2,1)}), bf16[8,96,2048]{2,1,0:T(8,128)(2,1)S(1)}, u32[]{:S(2)}, u32[]{:S(2)}) async-start(bf16[8,96,2048]{2,1,0:T(8,128)(2,1)} %bitcast.58), calls=%async_computation.3 | async-start | bytes 6291456 | tf_op jit(solution)/shard_map/all_to_all | solution.py:59
  52.9 139.4 %all-to-all-done.3 = bf16[8,96,2048]{2,1,0:T(8,128)(2,1)S(1)} async-done(((bf16[8,96,2048]{2,1,0:T(8,128)(2,1)}), bf16[8,96,2048]{2,1,0:T(8,128)(2,1)S(1)}, u32[]{:S(2)}, u32[]{:S(2)}) %all-to-all-start.3) | async-done | bytes 3145760 | tf_op jit(solution)/shard_map/all_to_all | solution.py:59
  196.9 9.7 %all-to-all-start.4 = ((bf16[256,2,1024]{2,0,1:T(8,128)(2,1)}), bf16[256,2,1024]{2,0,1:T(8,128)(2,1)}, u32[]{:S(2)}, u32[]{:S(2)}) async-start(bf16[256,2,1024]{2,0,1:T(8,128)(2,1)} %bitcast.46), calls=%async_computation.4 | async-start | bytes 2097152 | tf_op jit(solution)/shard_map/all_to_all | solution.py:30
  206.6 3.0 convert_reduce_fusion
  209.6 7.6 %all-to-all-done.4 = bf16[256,2,1024]{2,0,1:T(8,128)(2,1)} async-done(((bf16[256,2,1024]{2,0,1:T(8,128)(2,1)}), bf16[256,2,1024]{2,0,1:T(8,128)(2,1)}, u32[]{:S(2)}, u32[]{:S(2)}) %all-to-all-start.4) | async-done | bytes 1048608 | tf_op jit(solution)/shard_map/all_to_all | solution.py:30
  217.2 7.5 %convolution_convert_fusion = bf16[3200,1024]{1,0:T(8,128)(2,1)} fusion(bf16[512,1024]{1,0:T(8,128)(2,1)} %bitcast.16, bf16[512,3200]{0,1:T(8,128)(2,1)S(1)} %copy-done.2, f32[3200]{0:T(1024)S(1)} %copy-done.8, f32[3200]{0:T(1024)S(1)} %copy-done.7, f32[512]{0:T(512)S(1)} %get-tuple-element.17, f32[512]{0:T(512)S(1)} %get-tuple-element.16), kind=kOutput, calls=%fused_computation.5 | convolution fusion | flops 3368550400 | bytes 10908672 | tf_op jit(solution)/shard_map/dot_general | solution.py:65
  227.0 6.9 %convolution_convert_fusion.1 = bf16[512,3200]{1,0:T(8,128)(2,1)S(1)} fusion(bf16[512,1024]{1,0:T(8,128)(2,1)} %bitcast.16, bf16[3200,1024]{1,0:T(8,128)(2,1)} %all-gather.5.cloned.1.call-done), kind=kOutput, calls=%fused_computation.11 | convolution fusion | flops 3357081600 | bytes 10878976 | tf_op jit(solution)/shard_map/dot_general | solution.py:80
  233.9 3.4 copy.26
  237.4 3.9 all-to-all-start.5
  241.3 8.7 %convolution_convert_fusion.2 = bf16[512,1024]{1,0:T(8,128)(2,1)} fusion(bf16[3200,1024]{1,0:T(8,128)(2,1)} %all-gather.5.cloned.1.call-done, bf16[512,3200]{0,1:T(8,128)(2,1)} %all-gather.3.cloned.1.call-done, f32[3200]{0:T(1024)S(1)} %copy-done.8, f32[3200]{0:T(1024)S(1)} %copy-done.7, f32[512]{0:T(512)S(1)} %get-tuple-element.17, ...), kind=kOutput, calls=%fused_computation.18 | convolution fusion | flops 3365797888 | bytes 10908672 | tf_op jit(solution)/shard_map/dot_general | solution.py:75
  250.0 2.3 copy.23
  252.3 27.1 %all-to-all-done.5 = bf16[512,4,800]{0,2,1:T(8,128)(2,1)S(1)} async-done(((bf16[512,4,800]{0,2,1:T(8,128)(2,1)}), bf16[512,4,800]{0,2,1:T(8,128)(2,1)S(1)}, u32[]{:S(2)}, u32[]{:S(2)}) %all-to-all-start.5) | async-done | bytes 3276832 | tf_op jit(solution)/shard_map/all_to_all | solution.py:85
  279.4 4.4 all-to-all-start.1
  287.5 10.1 %all-to-all-done.1 = bf16[2,256,1024]{1,2,0:T(8,128)(2,1)} async-done(((bf16[2,256,1024]{1,2,0:T(8,128)(2,1)}), bf16[2,256,1024]{1,2,0:T(8,128)(2,1)}, u32[]{:S(2)}, u32[]{:S(2)}) %all-to-all-start.1) | async-done | bytes 1048608 | tf_op jit(solution)/shard_map/all_to_all | solution.py:30
  297.6 3.5 all-to-all-start.6
  302.6 4.3 scatter_custom_fusion
  306.9 4.6 all-to-all-done.6
  312.4 9.3 %all-to-all-start.2 = ((bf16[8,96,2048]{2,1,0:T(8,128)(2,1)}), bf16[8,96,2048]{2,1,0:T(8,128)(2,1)S(1)}, u32[]{:S(2)}, u32[]{:S(2)}) async-start(bf16[8,96,2048]{2,1,0:T(8,128)(2,1)} %bitcast.52), calls=%async_computation.2 | async-start | bytes 6291456 | tf_op jit(solution)/shard_map/all_to_all | solution.py:59
  325.8 87.7 %all-to-all-done.2 = bf16[8,96,2048]{2,1,0:T(8,128)(2,1)S(1)} async-done(((bf16[8,96,2048]{2,1,0:T(8,128)(2,1)}), bf16[8,96,2048]{2,1,0:T(8,128)(2,1)S(1)}, u32[]{:S(2)}, u32[]{:S(2)}) %all-to-all-start.2) | async-done | bytes 3145760 | tf_op jit(solution)/shard_map/all_to_all | solution.py:59
  413.5 4.6 all-to-all-start.7
  422.8 8.2 %all-reduce.1 = (f32[256]{0:T(256)}, f32[256]{0:T(256)}) all-reduce(f32[256]{0:T(256)} %get-tuple-element.8, f32[256]{0:T(256)} %get-tuple-element.9), channel_id=1, replica_groups=mesh['enc'=8,'section'=2,'llmdp'=2] {'section','llmdp'}, use_global_device_ids=true, to_apply=%region_11.12 | all-reduce | flops 512 | bytes 4096 | tf_op jit(solution)/shard_map/psum | solution.py:90
  431.0 20.9 %all-reduce = (f32[800]{0:T(1024)}, f32[800]{0:T(1024)}) all-reduce(f32[800]{0:T(1024)} %get-tuple-element.7, f32[800]{0:T(1024)} %get-tuple-element.10), channel_id=1, replica_groups=mesh['enc'=8,'section'=2,'llmdp'=2] {'enc'}, use_global_device_ids=true, to_apply=%region_14.15 | all-reduce | flops 1600 | bytes 12800 | tf_op jit(solution)/shard_map/psum | solution.py:107
  (53 shorter events, 32.5 us)
Async XLA Ops:
  7.2 199.4 %all-gather.3.cloned.1.call-start = ((), (), s32[]{:S(2)}) async-start(), calls=%async_computation.9 | async-start | bytes 4096000 | tf_op jit(solution)/shard_map/all_gather | solution.py:39
  22.4 204.6 %all-gather.5.cloned.1.call-start = ((), (), s32[]{:S(2)}) async-start(), calls=%async_computation.10 | async-start | bytes 8192000 | tf_op jit(solution)/shard_map/all_gather | solution.py:36
  47.0 4.9 %copy-start.4 = (s32[256,1]{0,1:T(1,128)S(1)}, s32[256,1]{0,1:T(1,128)}, u32[]{:S(2)}) copy-start(s32[256,1]{0,1:T(1,128)} %param.10) | copy-start | bytes 3076
  47.0 145.3 %all-to-all-start.3 = ((bf16[8,96,2048]{2,1,0:T(8,128)(2,1)}), bf16[8,96,2048]{2,1,0:T(8,128)(2,1)S(1)}, u32[]{:S(2)}, u32[]{:S(2)}) async-start(bf16[8,96,2048]{2,1,0:T(8,128)(2,1)} %bitcast.58), calls=%async_computation.3 | async-start | bytes 6291456 | tf_op jit(solution)/shard_map/all_to_all | solution.py:59
  194.6 22.6 %copy-start.7 = (f32[3200]{0:T(1024)S(1)}, f32[3200]{0:T(1024)}, u32[]{:S(2)}) copy-start(f32[3200]{0:T(1024)} %param.7) | copy-start | bytes 38404
  194.6 22.6 %copy-start.8 = (f32[3200]{0:T(1024)S(1)}, f32[3200]{0:T(1024)}, u32[]{:S(2)}) copy-start(f32[3200]{0:T(1024)} %param.8) | copy-start | bytes 38404
  196.9 20.3 %all-to-all-start.4 = ((bf16[256,2,1024]{2,0,1:T(8,128)(2,1)}), bf16[256,2,1024]{2,0,1:T(8,128)(2,1)}, u32[]{:S(2)}, u32[]{:S(2)}) async-start(bf16[256,2,1024]{2,0,1:T(8,128)(2,1)} %bitcast.46), calls=%async_computation.4 | async-start | bytes 2097152 | tf_op jit(solution)/shard_map/all_to_all | solution.py:30
  206.6 206.9 %reduce-scatter.2.cloned.1.call-start = ((), (), s32[]{:S(2)}) async-start(), calls=%async_computation.11 | async-start | bytes 8192000 | tf_op jit(solution)/shard_map/reduce_scatter | solution.py:64
  206.6 10.6 %copy-start.2 = (bf16[512,3200]{0,1:T(8,128)(2,1)S(1)}, bf16[512,3200]{0,1:T(8,128)(2,1)}, u32[]{:S(2)}) copy-start(bf16[512,3200]{0,1:T(8,128)(2,1)} %all-gather.3.cloned.1.call-done) | copy-start | bytes 9830404
  209.6 31.7 %copy-start.5 = (f32[512]{0:T(512)}, f32[512]{0:T(512)S(1)}, u32[]{:S(2)}) copy-start(f32[512]{0:T(512)S(1)} %get-tuple-element.17) | copy-start | bytes 6148
  209.6 31.7 %copy-start.6 = (f32[512]{0:T(512)}, f32[512]{0:T(512)S(1)}, u32[]{:S(2)}) copy-start(f32[512]{0:T(512)S(1)} %get-tuple-element.16) | copy-start | bytes 6148
  237.4 42.0 %all-to-all-start.5 = ((bf16[512,4,800]{0,2,1:T(8,128)(2,1)}), bf16[512,4,800]{0,2,1:T(8,128)(2,1)S(1)}, u32[]{:S(2)}, u32[]{:S(2)}) async-start(bf16[512,4,800]{0,2,1:T(8,128)(2,1)} %bitcast.50), calls=%async_computation.5 | async-start | bytes 6553600 | tf_op jit(solution)/shard_map/all_to_all | solution.py:85
  279.4 18.2 %all-to-all-start.1 = ((bf16[2,256,1024]{1,2,0:T(8,128)(2,1)}), bf16[2,256,1024]{1,2,0:T(8,128)(2,1)}, u32[]{:S(2)}, u32[]{:S(2)}) async-start(bf16[2,256,1024]{1,2,0:T(8,128)(2,1)} %copy.23), calls=%async_computation.1 | async-start | bytes 2097152 | tf_op jit(solution)/shard_map/all_to_all | solution.py:30
  297.6 13.9 %all-to-all-start.6 = ((bf16[2,256,800]{1,2,0:T(8,128)(2,1)}), bf16[2,256,800]{1,2,0:T(8,128)(2,1)S(1)}, u32[]{:S(2)}, u32[]{:S(2)}) async-start(bf16[2,256,800]{1,2,0:T(8,128)(2,1)} %bitcast.47), calls=%async_computation.6 | async-start | bytes 1638400 | tf_op jit(solution)/shard_map/all_to_all | solution.py:30
  311.5 0.9 copy-start.3
  312.4 101.1 %all-to-all-start.2 = ((bf16[8,96,2048]{2,1,0:T(8,128)(2,1)}), bf16[8,96,2048]{2,1,0:T(8,128)(2,1)S(1)}, u32[]{:S(2)}, u32[]{:S(2)}) async-start(bf16[8,96,2048]{2,1,0:T(8,128)(2,1)} %bitcast.52), calls=%async_computation.2 | async-start | bytes 6291456 | tf_op jit(solution)/shard_map/all_to_all | solution.py:59
  321.7 99.4 %copy-start.1 = (bf16[256,800]{0,1:T(8,128)(2,1)S(1)}, bf16[256,800]{0,1:T(8,128)(2,1)}, u32[]{:S(2)}) copy-start(bf16[256,800]{0,1:T(8,128)(2,1)} %param.6) | copy-start | bytes 1228804
  413.5 41.2 %all-to-all-start.7 = ((bf16[2,400,1024]{2,1,0:T(8,128)(2,1)}), bf16[2,400,1024]{2,1,0:T(8,128)(2,1)}, u32[]{:S(2)}, u32[]{:S(2)}) async-start(bf16[2,400,1024]{2,1,0:T(8,128)(2,1)} %bitcast.60), calls=%async_computation.8 | async-start | bytes 3276800 | tf_op jit(solution)/shard_map/all_to_all | solution.py:30
  420.2 0.9 copy-start
Sparse Core Ops, SparseCore 0:
  22.5 29.5 all-gather.2
  53.7 173.2 all-gather.4
  229.3 138.2 reduce-scatter.1
